TPU v7x, 32 devices: a whole 2x2x4 slice. The times are simulated.
32 devices in a mesh: rep: 2 (over x), shard: 16 (over z, y, core).
Axes of the slice: x: 2, y: 2, z: 4, core: 2. Of those that a mesh axis runs over, the one named last changes fastest.
Arguments:
- features: float32 [16384, 256], P(('rep', 'shard')), may hold values from -6 to 6
- seed_self: float32 [4096, 256], P(('rep', 'shard')), may hold values from -6 to 6
- hub_ids: int32 [4096], P(('rep', 'shard')), may hold values from 0 to 511
- requests: int32 [512, 32], P(('rep', 'shard')), may hold values from 0 to 511
- counts: int32 [512], P(('rep', 'shard')), may hold values from 1 to 32, as said below
- neighbors: int32 [4096, 15], P(('rep', 'shard')), may hold values from 0 to 767
- weight: float32 [256, 256], replicated, may hold values from -1 to 1
- out_bias: float32 [256], replicated, may hold values from -4 to 4
Outputs:
- embedded: float32 [4096, 256], P(('rep', 'shard'))
Inputs may be any that keep to these rules, and one draw needn't show every extreme that they name: `hub_ids`: offsets into the block of features of the same device. `requests`: row d of a device's lists holds offsets into the block of features of the device at shard index d with the same rep index; empty slots hold offsets too. counts[r, s, d] slots of the list from shard index s to shard index d are live, the first ones; for every rep index some destination has 32 live slots from every source. `neighbors`: A code below 256 names a row of the device's hub cache; a code 256 + d * 32 + c names slot c of the device's list to shard index d, and counts only where that slot is live.
All inputs are finite; a program needn't handle non-finite values.
Results may differ from a plain program's by a relative error of at most 0.0003.
Values sent between devices are 32-bit elements; how exact they have to be, the bound alone decides.
A program may use at most 64 MiB of HBM per device.

v0:
```python
import math

import jax
import jax.numpy as jnp
from jax import lax
from jax.sharding import PartitionSpec as P


def count_product(rows, codes, offset, row_scale):
    seed_count, fanout = codes.shape
    block_size = math.gcd(seed_count, 128)
    row_count = rows.shape[0]
    code_iota = lax.broadcasted_iota(jnp.int32, (1, row_count), 1) + offset

    def per_block(block_codes):
        tally = jnp.zeros((block_size, row_count), jnp.float32)
        for column in range(fanout):
            tally = tally + (block_codes[:, column : column + 1] == code_iota).astype(jnp.float32)
        tally = tally * row_scale[None, :]
        return jnp.dot(
            tally, rows, precision=lax.Precision.HIGHEST, preferred_element_type=jnp.float32
        )

    summed = lax.map(per_block, codes.reshape(-1, block_size, fanout))
    return summed.reshape(seed_count, rows.shape[1])


def project(values, weight):
    return jnp.dot(
        values, weight, precision=lax.Precision.HIGHEST, preferred_element_type=jnp.float32
    )


def local(features, seed_self, hub_ids, requests, counts, neighbors, weight, out_bias):
    shard_count = lax.axis_size("shard")
    capacity = requests.shape[1]
    feat_width = features.shape[1]
    hub_total = hub_ids.shape[0] * lax.axis_size("rep")
    local_hubs = jnp.take(features, hub_ids, axis=0)
    slot_index = lax.broadcasted_iota(jnp.int32, (shard_count, capacity), 1)
    slot_live = (slot_index < counts[:, None]).astype(jnp.float32).reshape(-1)
    code_live = jnp.concatenate([jnp.ones((hub_total,), jnp.float32), slot_live])
    weights = jnp.take(code_live, neighbors)
    taken = 1.0 + jnp.sum(weights, axis=1)
    hub_rows = lax.all_gather(local_hubs, "rep", axis=0, tiled=True)
    hub_part = count_product(hub_rows, neighbors, 0, jnp.ones((hub_total,), jnp.float32))
    looked = jnp.take(
        features, lax.all_to_all(requests, "shard", split_axis=0, concat_axis=0, tiled=True), axis=0
    )
    fetched = lax.all_to_all(looked, "shard", split_axis=0, concat_axis=0, tiled=True)
    slot_rows = fetched.reshape(-1, feat_width)
    slot_part = count_product(slot_rows, neighbors, hub_total, slot_live)
    total = seed_self + (hub_part + slot_part)
    mean_rows = total / taken[:, None]
    product = project(mean_rows, weight)
    return jnp.maximum(product + out_bias, 0.0)


def solution(mesh):
    return jax.shard_map(
        local,
        mesh=mesh,
        in_specs=(
            P(("rep", "shard"), None),
            P(("rep", "shard"), None),
            P(("rep", "shard")),
            P(("rep", "shard"), None),
            P(("rep", "shard")),
            P(("rep", "shard"), None),
            P(),
            P(),
        ),
        out_specs=P(("rep", "shard"), None),
        check_vma=False,
    )
```

profile of v0, /device:TPU:0, one launch (start us, length us, event | category | flops | bytes accessed | tf_op | source)
XLA Modules:
  0.0 37.0 jit_solution(1455155119561866945)
XLA Ops:
  0.0 0.0 copy-start
  0.0 0.0 copy-start.6
  0.0 7.5 %all-to-all-start = ((s32[16,1,32]{2,1,0:T(1,128)}), s32[16,1,32]{2,1,0:T(1,128)S(1)}, u32[]{:S(2)}, u32[]{:S(2)}) async-start(s32[16,1,32]{2,1,0:T(1,128)} %bitcast.45), calls=%async_computation | async-start | bytes 16384 | tf_op jit(solution)/shard_map/all_to_all | solution.py:48
  7.6 0.0 copy-done.6
  7.6 0.0 copy-start.2
  7.6 0.6 %copy-done.2 = s32[128,15]{0,1:T(8,128)S(1)} copy-done((s32[128,15]{0,1:T(8,128)S(1)}, s32[128,15]{0,1:T(8,128)}, u32[]{:S(2)}) %copy-start.2) | copy-done | bytes 7704
  8.3 0.0 copy-done
  8.3 0.8 %gather_fusion = f32[128,256]{1,0:T(8,128)S(1)} fusion(f32[512,256]{1,0:T(8,128)S(1)} %copy-done, s32[1024]{0:T(1024)S(1)} %pad_clamp_fusion.2), kind=kCustom, calls=%fused_computation | custom fusion | bytes 262656 | tf_op jit(solution)/shard_map/jit(_take)/gather | solution.py:39
  9.0 0.0 copy-start.4
  9.0 0.1 broadcast_select_fusion.1
  9.1 0.6 %copy-done.4 = s32[16]{0:T(128)S(1)} copy-done((s32[16]{0:T(128)S(1)}, s32[16]{0:T(128)}, u32[]{:S(2)}) %copy-start.4) | copy-done | bytes 88
  9.7 0.1 fusion.110
  9.8 0.1 copy.19
  9.9 0.2 reshape.107
  10.1 3.8 %all-to-all-done = s32[16,1,32]{2,1,0:T(1,128)S(1)} async-done(((s32[16,1,32]{2,1,0:T(1,128)}), s32[16,1,32]{2,1,0:T(1,128)S(1)}, u32[]{:S(2)}, u32[]{:S(2)}) %all-to-all-start) | async-done | bytes 2080 | tf_op jit(solution)/shard_map/all_to_all | solution.py:48
  13.9 0.1 reshape.99
  14.0 1.6 %gather_fusion.1 = f32[512,256]{1,0:T(8,128)S(1)} fusion(f32[512,256]{1,0:T(8,128)S(1)} %copy-done, s32[1024]{0:T(1024)S(1)} %pad_clamp_fusion.1), kind=kCustom, calls=%fused_computation.1 | custom fusion | bytes 1050624 | tf_op jit(solution)/shard_map/jit(_take)/gather | solution.py:47
  15.6 0.9 %broadcast_select_fusion = f32[16,32,256]{2,1,0:T(8,128)} fusion(f32[16,32,256]{2,1,0:T(8,128)S(1)} %bitcast.41, pred[16,32]{1,0:T(8,128)(4,1)S(1)} %compare_and_fusion), kind=kLoop, calls=%fused_computation.8 | loop fusion | flops 131072 | bytes 1049088 | tf_op jit(solution)/shard_map/jit(_take)/select_n | solution.py:47
  16.5 3.6 %all-to-all-start.1 = ((f32[16,32,256]{2,1,0:T(8,128)}), f32[16,32,256]{2,1,0:T(8,128)S(1)}, u32[]{:S(2)}, u32[]{:S(2)}) async-start(f32[16,32,256]{2,1,0:T(8,128)} %broadcast_select_fusion), calls=%async_computation.1 | async-start | bytes 1048576 | tf_op jit(solution)/shard_map/all_to_all | solution.py:50
  20.1 0.1 reshape.88
  20.2 7.2 %gather_fusion.2 = f32[1920]{0:T(1024)S(1)} fusion(f32[768]{0:T(1024)S(1)} %concatenate.3, s32[2048]{0:T(1024)S(1)} %pad_clamp_fusion), kind=kCustom, calls=%fused_computation.2 | custom fusion | bytes 23040 | tf_op jit(solution)/shard_map/jit(_take)/gather | solution.py:43
  27.4 0.2 reshape.106
  27.6 0.1 copy.20
  27.7 6.4 %all_gather.3 = f32[256,256]{1,0:T(8,128)S(1)} all-gather(f32[128,256]{1,0:T(8,128)S(1)} %broadcast_select_fusion.1), channel_id=1, replica_groups=mesh['rep'=2,'shard'=16] {'rep'}, dimensions={0}, use_global_device_ids=true | all-gather | bytes 393216 | tf_op jit(solution)/shard_map/all_gather | solution.py:45
  34.1 0.0 copy-start.5
  34.1 0.9 %fusion.50 = f32[128,256]{1,0:T(8,128)S(1)} fusion(f32[256,256]{1,0:T(8,128)S(1)} %all_gather.3, s32[128]{0:T(128)S(1)} %get-tuple-element.52, s32[128]{0:T(128)S(1)} %get-tuple-element.25, s32[128]{0:T(128)S(1)} %get-tuple-element.32, s32[128]{0:T(128)S(1)} %get-tuple-element.33, s32[128]{0:T(128)S(1)} %get-tuple-element.34, ...), kind=kOutput, calls=%fused_computation.56 | convolution fusion | flops 102105088 | bytes 400896 | tf_op jit(solution)/shard_map/while/body/eval_jaxpr/dot_general | solution.py:20
  35.0 0.0 all-to-all-done.1
  35.0 0.0 copy-done.5
  35.1 0.0 copy-start.1
  35.1 0.0 copy-start.3
  35.1 0.9 %fusion.2 = f32[128,256]{1,0:T(8,128)S(1)} fusion(f32[128,256]{1,0:T(8,128)S(1)} %copy-done.5, f32[128,256]{1,0:T(8,128)S(1)} %fusion.50, f32[512,256]{1,0:T(8,128)S(1)} %bitcast.42, f32[512]{0:T(512)S(1)} %reshape.88, s32[512]{0:T(512)S(1)} %iota_add_fusion, s32[128]{0:T(128)S(1)} %get-tuple-element.52, s32[128]{0:T(128)S(1)} %get-tuple-element.25, ...), kind=kOutput, calls=%fused_computation.7 | convolution fusion | flops 204374016 | bytes 929792 | tf_op jit(solution)/shard_map/while/body/eval_jaxpr/dot_general | solution.py:20
  35.9 0.1 copy-done.1
  36.0 0.0 copy-done.3
  36.0 0.9 %fusion = f32[128,256]{1,0:T(8,128)} fusion(f32[128,256]{1,0:T(8,128)S(1)} %fusion.2, f32[256,256]{1,0:T(8,128)S(1)} %copy-done.1, f32[256]{0:T(256)S(1)} %copy-done.3), kind=kOutput, calls=%fused_computation.4 | convolution fusion | flops 100728832 | bytes 525312 | tf_op jit(solution)/shard_map/dot_general | solution.py:29
  (13 shorter events, 0.1 us)
Async XLA Ops:
  0.0 8.3 %copy-start = (f32[512,256]{1,0:T(8,128)S(1)}, f32[512,256]{1,0:T(8,128)}, u32[]{:S(2)}) copy-start(f32[512,256]{1,0:T(8,128)} %param.8) | copy-start | bytes 1572868
  0.0 7.6 %copy-start.6 = (s32[128]{0:T(128)S(1)}, s32[128]{0:T(128)}, u32[]{:S(2)}) copy-start(s32[128]{0:T(128)} %param.10) | copy-start | bytes 1540
  0.0 13.9 %all-to-all-start = ((s32[16,1,32]{2,1,0:T(1,128)}), s32[16,1,32]{2,1,0:T(1,128)S(1)}, u32[]{:S(2)}, u32[]{:S(2)}) async-start(s32[16,1,32]{2,1,0:T(1,128)} %bitcast.45), calls=%async_computation | async-start | bytes 16384 | tf_op jit(solution)/shard_map/all_to_all | solution.py:48
  7.6 0.7 %copy-start.2 = (s32[128,15]{0,1:T(8,128)S(1)}, s32[128,15]{0,1:T(8,128)}, u32[]{:S(2)}) copy-start(s32[128,15]{0,1:T(8,128)} %param.13) | copy-start | bytes 23044
  9.0 0.7 %copy-start.4 = (s32[16]{0:T(128)S(1)}, s32[16]{0:T(128)}, u32[]{:S(2)}) copy-start(s32[16]{0:T(128)} %param.12) | copy-start | bytes 196
  16.5 18.5 %all-to-all-start.1 = ((f32[16,32,256]{2,1,0:T(8,128)}), f32[16,32,256]{2,1,0:T(8,128)S(1)}, u32[]{:S(2)}, u32[]{:S(2)}) async-start(f32[16,32,256]{2,1,0:T(8,128)} %broadcast_select_fusion), calls=%async_computation.1 | async-start | bytes 1048576 | tf_op jit(solution)/shard_map/all_to_all | solution.py:50
  34.1 0.9 %copy-start.5 = (f32[128,256]{1,0:T(8,128)S(1)}, f32[128,256]{1,0:T(8,128)}, u32[]{:S(2)}) copy-start(f32[128,256]{1,0:T(8,128)} %param.9) | copy-start | bytes 393220
  35.1 1.0 %copy-start.1 = (f32[256,256]{1,0:T(8,128)S(1)}, f32[256,256]{1,0:T(8,128)}, u32[]{:S(2)}) copy-start(f32[256,256]{1,0:T(8,128)} %param.14) | copy-start | bytes 786436
  35.1 0.9 %copy-start.3 = (f32[256]{0:T(256)S(1)}, f32[256]{0:T(256)}, u32[]{:S(2)}) copy-start(f32[256]{0:T(256)} %param.15) | copy-start | bytes 3076
where the time goes:
time: 37.3 us; the launch traced here: 37 us
  local copies, waits for them, and re-layouts  11.6 us (31%)
  starting transfers between devices  11.1 us (30%)
  blocking collectives  6.37 us (17%)
  waiting for transfers between devices  3.84 us (10%)
  matrix products  2.69 us (7%)
  other arithmetic  1.17 us (3%)
    all_to_all x1, starting transfers between devices, local(): lax.all_to_all(requests, 'shard', split_axis=0, concat_axis=0, tiled=True)  7.55 us
    gather x3, local copies, waits for them, and re-layouts, local(): weights = jnp.take(code_live, neighbors)  7.47 us
    all_gather x1, blocking collectives, local(): hub_rows = lax.all_gather(local_hubs, 'rep', axis=0, tiled=True)  6.37 us
    all_to_all x1, waiting for transfers between devices, local(): lax.all_to_all(requests, 'shard', split_axis=0, concat_axis=0, tiled=True)  3.84 us
    all_to_all x1, starting transfers between devices, local(): lax.all_to_all(looked, 'shard', split_axis=0, concat_axis=0, tiled=True)  3.57 us
    dot_general x2, matrix products, per_block(): jnp.dot(tally, rows, precision=lax.Precision.HIGHEST, preferred_element_t...  1.75 us
    gather x1, local copies, waits for them, and re-layouts, local(): jnp.take(features, lax.all_to_all(requests, 'shard', split_axis=0, concat...  1.57 us
    unnamed x14, local copies, waits for them, and re-layouts  1.31 us
  transfers between devices with their start and end apart: 2, of which 1 were waited for; matrix products, arithmetic and copies ran while one was open for 26% of the time, Pallas kernels for 0%

commit v1 on v0

v1 whole, which is shorter than its diff:
```python
import functools

import jax
import jax.numpy as jnp
from jax import lax
from jax.experimental import pallas as pl
from jax.experimental.pallas import tpu as pltpu
from jax.sharding import PartitionSpec as P

LANES = 128


def halves(values):
    high = values.astype(jnp.bfloat16)
    low = (values - high.astype(jnp.float32)).astype(jnp.bfloat16)
    return high, low


def dot(left, right):
    return jnp.dot(left, right, preferred_element_type=jnp.float32)


def columns_of(rows):
    count = rows.shape[0]
    if count < LANES:
        rows = jnp.concatenate([rows, jnp.zeros((LANES - count, LANES), rows.dtype)], axis=0)
    return rows.T


def kernel(
    n, reps, feat_hbm, self_hbm, hub_ref, req_ref, cnt_ref, nbr_ref, weight_hbm, out_ref,
    feat, own, weight, req_send, req_recv, gathered, fetched, hubs,
    local_sem, req_send_sem, req_recv_sem, row_send_sem, row_recv_sem, hub_send_sem, hub_recv_sem,
):
    me = lax.axis_index("shard")
    rep = lax.axis_index("rep")
    rows, width = feat.shape
    cap = req_ref.shape[1]
    hub_dev = hub_ref.shape[1]
    seeds, fanout = nbr_ref.shape
    hub_total = hub_dev * reps

    loads = [
        pltpu.make_async_copy(src, dst, local_sem.at[i])
        for i, (src, dst) in enumerate(((feat_hbm, feat), (weight_hbm, weight), (self_hbm, own)))
    ]
    for load in loads:
        load.start()

    barrier = pltpu.get_barrier_semaphore()
    for off in range(1, n):
        pl.semaphore_signal(barrier, inc=1, device_id={"shard": lax.rem(me + off, n)})
    for off in range(1, reps):
        pl.semaphore_signal(barrier, inc=1, device_id={"rep": lax.rem(rep + off, reps)})

    lists = jnp.concatenate([req_ref[...], jnp.zeros((n, LANES - cap), jnp.int32)], axis=1)
    req_send[...] = lists.reshape(n, 1, LANES)
    req_recv[0] = req_send[me]
    pl.semaphore_wait(barrier, n - 1 + reps - 1)

    asks = []
    for off in range(1, n):
        peer = lax.rem(me + off, n)
        ask = pltpu.make_async_remote_copy(
            src_ref=req_send.at[peer],
            dst_ref=req_recv.at[n - off],
            send_sem=req_send_sem.at[off],
            recv_sem=req_recv_sem.at[n - off],
            device_id={"shard": peer},
        )
        ask.start()
        asks.append(ask)

    loads[0].wait()
    high, low = halves(feat[...])
    row_iota = lax.broadcasted_iota(jnp.int32, (LANES, rows), 1)

    hub_columns = columns_of(jnp.broadcast_to(hub_ref[...], (8, hub_dev)))
    pick = (hub_columns[:, 0:1] == row_iota).astype(jnp.float32).astype(jnp.bfloat16)
    hubs[rep] = dot(pick, high) + dot(pick, low)
    shares = []
    for off in range(1, reps):
        share = pltpu.make_async_remote_copy(
            src_ref=hubs.at[rep],
            dst_ref=hubs.at[rep],
            send_sem=hub_send_sem.at[off],
            recv_sem=hub_recv_sem.at[rep],
            device_id={"rep": lax.rem(rep + off, reps)},
        )
        share.start()
        shares.append(share)

    code_count = hub_total + n * cap
    code_iota = lax.broadcasted_iota(jnp.int32, (seeds, code_count), 1)
    codes = nbr_ref[...]
    tally = jnp.zeros((seeds, code_count), jnp.float32)
    for k in range(fanout):
        tally = tally + (codes[:, k : k + 1] == code_iota).astype(jnp.float32)
    spread = (
        lax.broadcasted_iota(jnp.int32, (n, n * cap), 1) // cap
        == lax.broadcasted_iota(jnp.int32, (n, n * cap), 0)
    ).astype(jnp.float32).astype(jnp.bfloat16)
    fill = jnp.broadcast_to(cnt_ref[...].astype(jnp.float32), (8, n)).astype(jnp.bfloat16)
    slot_fill = dot(fill, spread)[0:1]
    slot_iota = (lax.broadcasted_iota(jnp.int32, (1, n * cap), 1) % cap).astype(jnp.float32)
    slot_live = (slot_iota < slot_fill).astype(jnp.float32)
    hub_tally = tally[:, :hub_total]
    slot_tally = tally[:, hub_total:] * slot_live
    taken = 1.0 + jnp.sum(hub_tally, axis=1, keepdims=True) + jnp.sum(slot_tally, axis=1, keepdims=True)
    scale = 1.0 / taken
    hub_tally = hub_tally.astype(jnp.bfloat16)
    slot_tally = slot_tally.astype(jnp.bfloat16)

    for off in range(1, n):
        asks[off - 1].wait_send()
        pltpu.make_async_copy(req_recv.at[off], req_recv.at[off], req_recv_sem.at[off]).wait()
    request_columns = columns_of(req_recv[...].reshape(n, LANES))
    replies = []
    batch = LANES // cap
    for first in range(0, n, batch):
        pick = jnp.concatenate(
            [
                (request_columns[:cap, off : off + 1] == row_iota[:cap]).astype(jnp.float32)
                for off in range(first, first + batch)
            ],
            axis=0,
        ).astype(jnp.bfloat16)
        gathered[first : first + batch] = (dot(pick, high) + dot(pick, low)).reshape(batch, cap, width)
        for off in range(first, first + batch):
            if off == 0:
                continue
            reply = pltpu.make_async_remote_copy(
                src_ref=gathered.at[off],
                dst_ref=fetched.at[me],
                send_sem=row_send_sem.at[off],
                recv_sem=row_recv_sem.at[me],
                device_id={"shard": lax.rem(me + off, n)},
            )
            reply.start()
            replies.append(reply)
    fetched[me] = gathered[0]

    loads[2].wait()
    for off in range(1, reps):
        shares[off - 1].wait_send()
        other = lax.rem(rep + off, reps)
        pltpu.make_async_copy(hubs.at[other], hubs.at[other], hub_recv_sem.at[other]).wait()
    hub_high, hub_low = halves(hubs[...].reshape(hub_total, width))
    total = own[...] + (dot(hub_tally, hub_high) + dot(hub_tally, hub_low))
    loads[1].wait()
    weight_high, weight_low = halves(weight[...])

    for off in range(1, n):
        owner = lax.rem(me + off, n)
        pltpu.make_async_copy(fetched.at[owner], fetched.at[owner], row_recv_sem.at[owner]).wait()
    row_high, row_low = halves(fetched[...].reshape(n * cap, width))
    total = total + (dot(slot_tally, row_high) + dot(slot_tally, row_low))
    mean_high, mean_low = halves(total * scale)
    out_ref[...] = dot(mean_high, weight_high) + (dot(mean_high, weight_low) + dot(mean_low, weight_high))
    for reply in replies:
        reply.wait_send()


def local(n, reps, features, seed_self, hub_ids, requests, counts, neighbors, weight, out_bias):
    rows, width = features.shape
    cap = requests.shape[1]
    hub_dev = hub_ids.shape[0]
    seeds = neighbors.shape[0]
    hbm = pl.BlockSpec(memory_space=pl.ANY)
    vmem = pl.BlockSpec(memory_space=pltpu.VMEM)
    dma = pltpu.SemaphoreType.DMA
    product = pl.pallas_call(
        functools.partial(kernel, n, reps),
        out_shape=jax.ShapeDtypeStruct((seeds, width), jnp.float32),
        in_specs=[hbm, hbm, vmem, vmem, vmem, vmem, hbm],
        out_specs=vmem,
        scratch_shapes=[
            pltpu.VMEM((rows, width), jnp.float32),
            pltpu.VMEM((seeds, width), jnp.float32),
            pltpu.VMEM(weight.shape, jnp.float32),
            pltpu.VMEM((n, 1, LANES), jnp.int32),
            pltpu.VMEM((n, 1, LANES), jnp.int32),
            pltpu.VMEM((n, cap, width), jnp.float32),
            pltpu.VMEM((n, cap, width), jnp.float32),
            pltpu.VMEM((reps, hub_dev, width), jnp.float32),
            dma((3,)),
            dma((n,)),
            dma((n,)),
            dma((n,)),
            dma((n,)),
            dma((reps,)),
            dma((reps,)),
        ],
        compiler_params=pltpu.CompilerParams(collective_id=0, has_side_effects=True),
    )(features, seed_self, hub_ids[None], requests, counts[None], neighbors, weight)
    return jnp.maximum(product + out_bias, 0.0)


def solution(mesh):
    return jax.shard_map(
        functools.partial(local, mesh.shape["shard"], mesh.shape["rep"]),
        mesh=mesh,
        in_specs=(
            P(("rep", "shard"), None),
            P(("rep", "shard"), None),
            P(("rep", "shard")),
            P(("rep", "shard"), None),
            P(("rep", "shard")),
            P(("rep", "shard"), None),
            P(),
            P(),
        ),
        out_specs=P(("rep", "shard"), None),
        check_vma=False,
    )
```

time: 37.3 us -> 26.6 us (0.71)
  the two profiles are of different devices: /device:TPU:0 before, /device:TPU:9 now
where the time goes in v1:
time: 26.6 us; the launch traced here: 26.4 us
  Pallas kernels  23.4 us (88%)
  other arithmetic  1.57 us (6%)
  local copies, waits for them, and re-layouts  1.43 us (5%)
    pallas_call x1, Pallas kernels, local(): pl.pallas_call(functools.partial(kernel, n, reps), out_shape=jax.ShapeDty...  23.4 us
    max x1, other arithmetic, local(): return jnp.maximum(product + out_bias, 0.0)  1.57 us
    unnamed x3, local copies, waits for them, and re-layouts  1.43 us

profile of v1, /device:TPU:9, one launch (start us, length us, event | category | flops | bytes accessed | tf_op | source)
XLA Modules:
  0.0 26.4 jit_solution(3614932043787320183)
XLA Ops:
  0.0 1.4 %copy.9.nbr_ref = s32[128,15]{1,0:T(8,128)} copy(s32[128,15]{0,1:T(8,128)} %param.13) | data formatting | bytes 15360 | tf_op args[5]
  1.4 0.0 copy-start
  1.4 23.4 %shard_map.82 = f32[128,256]{1,0:T(8,128)} custom-call(f32[512,256]{1,0:T(8,128)} %feat_hbm.1, f32[128,256]{1,0:T(8,128)} %self_hbm.1, s32[1,128]{1,0:T(1,128)} %bitcast.2, s32[16,32]{1,0:T(8,128)} %req_ref.1, s32[1,16]{1,0:T(1,128)} %bitcast.3, s32[128,15]{1,0:T(8,128)} %copy.9.nbr_ref, f32[256,256]{1,0:T(8,128)} %weight_hbm.1), custom_call_target="tpu_custom_call" | custom-call | tf_op jit(solution)/shard_map/pallas_call | solution.py:172
  24.8 0.0 copy-done
  24.8 1.6 %add_maximum_fusion = f32[128,256]{1,0:T(8,128)} fusion(f32[128,256]{1,0:T(8,128)} %shard_map.82, f32[256]{0:T(256)S(1)} %copy-done), kind=kLoop, calls=%fused_computation | loop fusion | flops 65536 | bytes 263168 | tf_op jit(solution)/shard_map/max | solution.py:196
Async XLA Ops:
  1.4 23.4 %copy-start = (f32[256]{0:T(256)S(1)}, f32[256]{0:T(256)}, u32[]{:S(2)}) copy-start(f32[256]{0:T(256)} %param.15) | copy-start | bytes 3076

commit v2 on v1

v2 whole, which is shorter than its diff:
```python
import functools

import jax
import jax.numpy as jnp
from jax import lax
from jax.experimental import pallas as pl
from jax.experimental.pallas import tpu as pltpu
from jax.sharding import PartitionSpec as P

LANES = 128


def halves(values):
    high = values.astype(jnp.bfloat16)
    low = (values - high.astype(jnp.float32)).astype(jnp.bfloat16)
    return high, low


def dot(left, right):
    return jnp.dot(left, right, preferred_element_type=jnp.float32)


def plan(me, n):
    quarter = n // 4
    block, place = me // quarter, lax.rem(me, quarter)
    side = block // 2
    outer = lax.rem(block + side, 2)
    inner_far = 2 - side
    outer_far = 3 - 3 * side
    sibling = block + 1 - 2 * lax.rem(block, 2)
    blocks = (inner_far, outer_far, sibling, block)
    peers = [[blocks[g] * quarter + lax.rem(place + q, quarter) for q in range(quarter)] for g in range(4)]
    mine = (1 - outer, 1 - outer, 2, 3)
    spots = [[mine[g] * quarter + (quarter - q) % quarter for q in range(quarter)] for g in range(4)]
    return blocks, sum(peers, []), sum(spots, [])


def columns_of(rows):
    count = rows.shape[0]
    if count < LANES:
        rows = jnp.concatenate([rows, jnp.zeros((LANES - count, LANES), rows.dtype)], axis=0)
    return rows.T


def kernel(
    n, reps, feat_hbm, self_hbm, hub_ref, req_ref, cnt_ref, nbr_ref, weight_hbm, out_ref,
    feat, own, weight, req_send, req_recv, gathered, fetched, hubs, slot_tally,
    local_sem, req_send_sem, req_recv_sem, row_send_sem, row_recv_sem, hub_send_sem, hub_recv_sem,
):
    me = lax.axis_index("shard")
    rep = lax.axis_index("rep")
    rows, width = feat.shape
    cap = req_ref.shape[1]
    hub_dev = hub_ref.shape[1]
    fanout, seeds = nbr_ref.shape
    hub_total = hub_dev * reps
    quarter = n // 4
    own_spot = n - quarter
    blocks, peers, spots = plan(me, n)
    others = [i for i in range(n) if i != own_spot]

    loads = [
        pltpu.make_async_copy(src, dst, local_sem.at[i])
        for i, (src, dst) in enumerate(((feat_hbm, feat), (weight_hbm, weight), (self_hbm, own)))
    ]
    for load in loads:
        load.start()

    barrier = pltpu.get_barrier_semaphore()
    for i in others:
        pl.semaphore_signal(barrier, inc=1, device_id={"shard": peers[i]})
    for off in range(1, reps):
        pl.semaphore_signal(barrier, inc=1, device_id={"rep": lax.rem(rep + off, reps)})

    lists = jnp.concatenate([req_ref[...], jnp.zeros((n, LANES - cap), jnp.int32)], axis=1)
    req_send[...] = lists.reshape(n, 1, LANES)
    req_recv[own_spot] = req_send[me]

    loads[0].wait()
    high, low = halves(feat[...])
    row_iota = lax.broadcasted_iota(jnp.int32, (LANES, rows), 1)
    hub_columns = columns_of(jnp.broadcast_to(hub_ref[...], (8, hub_dev)))
    pick = (hub_columns[:, 0:1] == row_iota).astype(jnp.float32).astype(jnp.bfloat16)
    hubs[rep] = dot(pick, high) + dot(pick, low)
    pl.semaphore_wait(barrier, n - 1 + reps - 1)

    asks = []
    for i in others:
        ask = pltpu.make_async_remote_copy(
            src_ref=req_send.at[peers[i]],
            dst_ref=req_recv.at[spots[i]],
            send_sem=req_send_sem.at[i],
            recv_sem=req_recv_sem.at[spots[i]],
            device_id={"shard": peers[i]},
        )
        ask.start()
        asks.append(ask)
    shares = []
    for off in range(1, reps):
        share = pltpu.make_async_remote_copy(
            src_ref=hubs.at[rep],
            dst_ref=hubs.at[rep],
            send_sem=hub_send_sem.at[off],
            recv_sem=hub_recv_sem.at[rep],
            device_id={"rep": lax.rem(rep + off, reps)},
        )
        share.start()
        shares.append(share)

    code_count = hub_total + n * cap
    code_iota = lax.broadcasted_iota(jnp.int32, (seeds, code_count), 1)
    codes = columns_of(nbr_ref[...])
    tally = jnp.zeros((seeds, code_count), jnp.float32)
    for k in range(fanout):
        tally = tally + (codes[:, k : k + 1] == code_iota).astype(jnp.float32)
    spread = (
        lax.broadcasted_iota(jnp.int32, (n, n * cap), 1) // cap
        == lax.broadcasted_iota(jnp.int32, (n, n * cap), 0)
    ).astype(jnp.float32).astype(jnp.bfloat16)
    fill = jnp.broadcast_to(cnt_ref[...].astype(jnp.float32), (8, n)).astype(jnp.bfloat16)
    slot_fill = dot(fill, spread)[0:1]
    slot_iota = (lax.broadcasted_iota(jnp.int32, (1, n * cap), 1) % cap).astype(jnp.float32)
    slot_live = (slot_iota < slot_fill).astype(jnp.float32)
    hub_tally = tally[:, :hub_total]
    live_tally = tally[:, hub_total:] * slot_live
    taken = 1.0 + jnp.sum(hub_tally, axis=1, keepdims=True) + jnp.sum(live_tally, axis=1, keepdims=True)
    scale = 1.0 / taken
    hub_tally = hub_tally.astype(jnp.bfloat16)
    for b in range(4):
        slot_tally[b] = live_tally[:, b * quarter * cap : (b + 1) * quarter * cap].astype(jnp.bfloat16)

    replies = []
    batch = min(LANES // cap, quarter)
    for group in range(4):
        span = range(group * quarter, (group + 1) * quarter)
        for i in span:
            if i != own_spot:
                pltpu.make_async_copy(req_recv.at[i], req_recv.at[i], req_recv_sem.at[i]).wait()
        request_columns = columns_of(req_recv[group * quarter : (group + 1) * quarter].reshape(quarter, LANES))
        for first in range(0, quarter, batch):
            pick = jnp.concatenate(
                [
                    (request_columns[:cap, q : q + 1] == row_iota[:cap]).astype(jnp.float32)
                    for q in range(first, first + batch)
                ],
                axis=0,
            ).astype(jnp.bfloat16)
            base = group * quarter + first
            gathered[base : base + batch] = (dot(pick, high) + dot(pick, low)).reshape(batch, cap, width)
            for i in range(base, base + batch):
                if i == own_spot:
                    continue
                reply = pltpu.make_async_remote_copy(
                    src_ref=gathered.at[i],
                    dst_ref=fetched.at[me],
                    send_sem=row_send_sem.at[i],
                    recv_sem=row_recv_sem.at[me],
                    device_id={"shard": peers[i]},
                )
                reply.start()
                replies.append(reply)
    fetched[me] = gathered[own_spot]
    for ask in asks:
        ask.wait_send()

    loads[2].wait()
    for off in range(1, reps):
        shares[off - 1].wait_send()
        other = lax.rem(rep + off, reps)
        pltpu.make_async_copy(hubs.at[other], hubs.at[other], hub_recv_sem.at[other]).wait()
    hub_high, hub_low = halves(hubs[...].reshape(hub_total, width))
    total = own[...] + (dot(hub_tally, hub_high) + dot(hub_tally, hub_low))
    loads[1].wait()
    weight_high, weight_low = halves(weight[...])

    for group in (3, 2, 0, 1):
        for i in range(group * quarter, (group + 1) * quarter):
            if i != own_spot:
                pltpu.make_async_copy(fetched.at[peers[i]], fetched.at[peers[i]], row_recv_sem.at[peers[i]]).wait()
        block = blocks[group]
        row_high, row_low = halves(fetched[pl.ds(block * quarter, quarter)].reshape(quarter * cap, width))
        counted = slot_tally[block]
        total = total + (dot(counted, row_high) + dot(counted, row_low))
    mean_high, mean_low = halves(total * scale)
    out_ref[...] = dot(mean_high, weight_high) + (dot(mean_high, weight_low) + dot(mean_low, weight_high))
    for reply in replies:
        reply.wait_send()


def local(n, reps, features, seed_self, hub_ids, requests, counts, neighbors, weight, out_bias):
    rows, width = features.shape
    cap = requests.shape[1]
    hub_dev = hub_ids.shape[0]
    seeds = neighbors.shape[0]
    hbm = pl.BlockSpec(memory_space=pltpu.HBM)
    vmem = pl.BlockSpec(memory_space=pltpu.VMEM)
    dma = pltpu.SemaphoreType.DMA
    product = pl.pallas_call(
        functools.partial(kernel, n, reps),
        out_shape=jax.ShapeDtypeStruct((seeds, width), jnp.float32),
        in_specs=[hbm, hbm, vmem, vmem, vmem, vmem, hbm],
        out_specs=vmem,
        scratch_shapes=[
            pltpu.VMEM((rows, width), jnp.float32),
            pltpu.VMEM((seeds, width), jnp.float32),
            pltpu.VMEM(weight.shape, jnp.float32),
            pltpu.VMEM((n, 1, LANES), jnp.int32),
            pltpu.VMEM((n, 1, LANES), jnp.int32),
            pltpu.VMEM((n, cap, width), jnp.float32),
            pltpu.VMEM((n, cap, width), jnp.float32),
            pltpu.VMEM((reps, hub_dev, width), jnp.float32),
            pltpu.VMEM((4, seeds, n // 4 * cap), jnp.bfloat16),
            dma((3,)),
            dma((n,)),
            dma((n,)),
            dma((n,)),
            dma((n,)),
            dma((reps,)),
            dma((reps,)),
        ],
        compiler_params=pltpu.CompilerParams(collective_id=0, has_side_effects=True),
    )(features, seed_self, hub_ids[None], requests, counts[None], neighbors.T, weight)
    return jnp.maximum(product + out_bias, 0.0)


def solution(mesh):
    return jax.shard_map(
        functools.partial(local, mesh.shape["shard"], mesh.shape["rep"]),
        mesh=mesh,
        in_specs=(
            P(("rep", "shard"), None),
            P(("rep", "shard"), None),
            P(("rep", "shard")),
            P(("rep", "shard"), None),
            P(("rep", "shard")),
            P(("rep", "shard"), None),
            P(),
            P(),
        ),
        out_specs=P(("rep", "shard"), None),
        check_vma=False,
    )
```

time: 26.6 us -> 26.8 us (level)
  the two profiles are of different devices: /device:TPU:9 before, /device:TPU:0 now
where the time goes in v2:
time: 26.8 us; the launch traced here: 26.6 us
  Pallas kernels  25 us (93%)
  other arithmetic  1.57 us (6%)
    pallas_call x1, Pallas kernels, local(): pl.pallas_call(functools.partial(kernel, n, reps), out_shape=jax.ShapeDty...  25 us
    max x1, other arithmetic, local(): return jnp.maximum(product + out_bias, 0.0)  1.57 us

profile of v2, /device:TPU:0, one launch (start us, length us, event | category | flops | bytes accessed | tf_op | source)
XLA Modules:
  0.0 26.6 jit_solution(2277058494378339480)
XLA Ops:
  0.0 0.0 copy-start
  0.0 25.0 %shard_map.82 = f32[128,256]{1,0:T(8,128)} custom-call(f32[512,256]{1,0:T(8,128)} %feat_hbm.1, f32[128,256]{1,0:T(8,128)} %self_hbm.1, s32[1,128]{1,0:T(1,128)} %bitcast.4, s32[16,32]{1,0:T(8,128)} %req_ref.1, s32[1,16]{1,0:T(1,128)} %bitcast.5, s32[15,128]{1,0:T(8,128)} %bitcast.3, f32[256,256]{1,0:T(8,128)} %weight_hbm.1), custom_call_target="tpu_custom_call" | custom-call | tf_op jit(solution)/shard_map/pallas_call | solution.py:198
  25.0 0.0 copy-done
  25.0 1.6 %add_maximum_fusion = f32[128,256]{1,0:T(8,128)} fusion(f32[128,256]{1,0:T(8,128)} %shard_map.82, f32[256]{0:T(256)S(1)} %copy-done), kind=kLoop, calls=%fused_computation | loop fusion | flops 65536 | bytes 263168 | tf_op jit(solution)/shard_map/max | solution.py:223
Async XLA Ops:
  0.0 25.0 %copy-start = (f32[256]{0:T(256)S(1)}, f32[256]{0:T(256)}, u32[]{:S(2)}) copy-start(f32[256]{0:T(256)} %param.15) | copy-start | bytes 3076

commit v3 on v1

v3 whole, which is shorter than its diff:
```python
import functools

import jax
import jax.numpy as jnp
from jax import lax
from jax.experimental import pallas as pl
from jax.experimental.pallas import tpu as pltpu
from jax.sharding import PartitionSpec as P

LANES = 128


def halves(values):
    high = values.astype(jnp.bfloat16)
    low = (values - high.astype(jnp.float32)).astype(jnp.bfloat16)
    return high, low


def dot(left, right):
    return jnp.dot(left, right, preferred_element_type=jnp.float32)


def columns_of(rows):
    count = rows.shape[0]
    if count < LANES:
        rows = jnp.concatenate([rows, jnp.zeros((LANES - count, LANES), rows.dtype)], axis=0)
    return rows.T


def kernel(
    n, reps, feat_hbm, self_hbm, hub_ref, req_ref, cnt_ref, nbr_ref, weight_hbm, out_ref,
    feat, own, weight, table, tables, req_recv, gathered, fetched, hubs, slot_tally,
    local_sem, ask_sem, req_recv_sem, table_send_sem, table_recv_sem, row_send_sem, row_recv_sem, hub_send_sem, hub_recv_sem,
):
    me = lax.axis_index("shard")
    rep = lax.axis_index("rep")
    rows, width = feat.shape
    cap = req_ref.shape[1]
    hub_dev = hub_ref.shape[1]
    fanout, seeds = nbr_ref.shape
    hub_total = hub_dev * reps
    quarter = n // 4
    block, place = me // quarter, lax.rem(me, quarter)
    side = block // 2
    inner = lax.rem(block + side, 2)
    is_inner = inner == 1
    near = 1 + lax.rem(block, 2)
    edge = 3 * side
    twin = 3 - block
    far = 3 - edge
    turns = [lax.rem(place + q, quarter) for q in range(quarter)]

    loads = [
        pltpu.make_async_copy(src, dst, local_sem.at[i])
        for i, (src, dst) in enumerate(((feat_hbm, feat), (weight_hbm, weight), (self_hbm, own)))
    ]
    for load in loads:
        load.start()

    barrier = pltpu.get_barrier_semaphore()

    def greet(peer_block, places):
        for spot in places:
            pl.semaphore_signal(barrier, inc=1, device_id={"shard": peer_block * quarter + spot})

    greet(block, turns[1:])
    greet(near, turns)

    @pl.when(is_inner)
    def _():
        greet(edge, turns)

    for off in range(1, reps):
        pl.semaphore_signal(barrier, inc=1, device_id={"rep": lax.rem(rep + off, reps)})

    lists = jnp.concatenate([req_ref[...], jnp.zeros((n, LANES - cap), jnp.int32)], axis=1)
    table[...] = lists.reshape(4, quarter, 1, LANES)
    req_recv[block, place] = table[block, place]
    pl.semaphore_wait(barrier, quarter - 1 + quarter + quarter * inner + reps - 1)

    def row_copies(source, owner_block, to_block, lane, places):
        return [
            pltpu.make_async_remote_copy(
                src_ref=source.at[to_block, spot],
                dst_ref=req_recv.at[owner_block, place],
                send_sem=ask_sem.at[lane, q],
                recv_sem=req_recv_sem.at[owner_block, place],
                device_id={"shard": to_block * quarter + spot},
            )
            for q, spot in enumerate(places)
        ]

    def table_copy(source, to_block, slot, lane):
        return pltpu.make_async_remote_copy(
            src_ref=source,
            dst_ref=tables.at[slot],
            send_sem=table_send_sem.at[lane],
            recv_sem=table_recv_sem.at[slot],
            device_id={"shard": to_block * quarter + place},
        )

    def start(copies):
        for copy in copies:
            copy.start()

    def sent(copies):
        for copy in copies:
            copy.wait_send()

    def table_wait(slot):
        pltpu.make_async_copy(tables.at[slot], tables.at[slot], table_recv_sem.at[slot]).wait()

    asks = row_copies(table, block, near, 0, turns) + row_copies(table, block, block, 1, turns[1:])
    edge_asks = row_copies(table, block, edge, 2, turns)
    own_table = table_copy(table, near, inner, 0)
    passed = [
        row_copies(tables.at[0], edge, twin, 3, turns) + [table_copy(tables.at[0], twin, 2, 1)],
        row_copies(tables.at[1], twin, edge, 4, turns),
        row_copies(tables.at[2], far, edge, 5, turns),
    ]

    own_table.start()
    start(asks)

    @pl.when(is_inner)
    def _():
        start(edge_asks)

    loads[0].wait()
    high, low = halves(feat[...])
    row_iota = lax.broadcasted_iota(jnp.int32, (LANES, rows), 1)

    @pl.when(is_inner)
    def _():
        for slot in (0, 1):
            table_wait(slot)
            start(passed[slot])

    batch = min(LANES // cap, quarter)

    def reply_copy(group, owner_block, q):
        spot = turns[q]
        return pltpu.make_async_remote_copy(
            src_ref=gathered.at[group, spot],
            dst_ref=fetched.at[me],
            send_sem=row_send_sem.at[group, q],
            recv_sem=row_recv_sem.at[me],
            device_id={"shard": owner_block * quarter + spot},
        )

    def unless_own(peer_block, q, action):
        if q:
            action()
        else:
            pl.when(peer_block != block)(action)

    def answer(group, peer_block):
        for q, spot in enumerate(turns):
            ref = req_recv.at[peer_block, spot]
            unless_own(peer_block, q, pltpu.make_async_copy(ref, ref, req_recv_sem.at[peer_block, spot]).wait)
        request_columns = columns_of(req_recv[peer_block].reshape(quarter, LANES))
        for first in range(0, quarter, batch):
            pick = jnp.concatenate(
                [
                    (request_columns[:cap, q : q + 1] == row_iota[:cap]).astype(jnp.float32)
                    for q in range(first, first + batch)
                ],
                axis=0,
            ).astype(jnp.bfloat16)
            picked = dot(pick, high) + dot(pick, low)
            gathered[group, first : first + batch] = picked.reshape(batch, cap, width)
        for q in range(quarter):
            unless_own(peer_block, q, reply_copy(group, peer_block, q).start)

    peer_blocks = (near, edge, 2 - lax.rem(block, 2), far)
    own_group = 1 + inner
    for group in range(3):
        answer(group, peer_blocks[group])

    @pl.when(is_inner)
    def _():
        table_wait(2)
        start(passed[2])

    answer(3, peer_blocks[3])
    fetched[me] = gathered[own_group, place]

    hub_columns = columns_of(jnp.broadcast_to(hub_ref[...], (8, hub_dev)))
    pick = (hub_columns[:, 0:1] == row_iota).astype(jnp.float32).astype(jnp.bfloat16)
    hubs[rep] = dot(pick, high) + dot(pick, low)
    shares = []
    for off in range(1, reps):
        share = pltpu.make_async_remote_copy(
            src_ref=hubs.at[rep],
            dst_ref=hubs.at[rep],
            send_sem=hub_send_sem.at[off],
            recv_sem=hub_recv_sem.at[rep],
            device_id={"rep": lax.rem(rep + off, reps)},
        )
        share.start()
        shares.append(share)

    code_count = hub_total + n * cap
    code_iota = lax.broadcasted_iota(jnp.int32, (seeds, code_count), 1)
    codes = columns_of(nbr_ref[...])
    tally = jnp.zeros((seeds, code_count), jnp.float32)
    for k in range(fanout):
        tally = tally + (codes[:, k : k + 1] == code_iota).astype(jnp.float32)
    spread = (
        lax.broadcasted_iota(jnp.int32, (n, n * cap), 1) // cap
        == lax.broadcasted_iota(jnp.int32, (n, n * cap), 0)
    ).astype(jnp.float32).astype(jnp.bfloat16)
    fill = jnp.broadcast_to(cnt_ref[...].astype(jnp.float32), (8, n)).astype(jnp.bfloat16)
    slot_fill = dot(fill, spread)[0:1]
    slot_iota = (lax.broadcasted_iota(jnp.int32, (1, n * cap), 1) % cap).astype(jnp.float32)
    slot_live = (slot_iota < slot_fill).astype(jnp.float32)
    hub_tally = tally[:, :hub_total]
    live_tally = tally[:, hub_total:] * slot_live
    taken = 1.0 + jnp.sum(hub_tally, axis=1, keepdims=True) + jnp.sum(live_tally, axis=1, keepdims=True)
    scale = 1.0 / taken
    hub_tally = hub_tally.astype(jnp.bfloat16)
    for b in range(4):
        slot_tally[b] = live_tally[:, b * quarter * cap : (b + 1) * quarter * cap].astype(jnp.bfloat16)

    own_table.wait_send()
    sent(asks)

    @pl.when(is_inner)
    def _():
        sent(edge_asks)
        for copies in passed:
            sent(copies)

    loads[2].wait()
    for off in range(1, reps):
        shares[off - 1].wait_send()
        other = lax.rem(rep + off, reps)
        pltpu.make_async_copy(hubs.at[other], hubs.at[other], hub_recv_sem.at[other]).wait()
    hub_high, hub_low = halves(hubs[...].reshape(hub_total, width))
    total = own[...] + (dot(hub_tally, hub_high) + dot(hub_tally, hub_low))
    loads[1].wait()
    weight_high, weight_low = halves(weight[...])

    for owner_block in (block, block + 1 - 2 * lax.rem(block, 2), 2 - side, far):
        for q, spot in enumerate(turns):
            ref = fetched.at[owner_block * quarter + spot]
            unless_own(owner_block, q, pltpu.make_async_copy(ref, ref, row_recv_sem.at[owner_block * quarter + spot]).wait)
        row_high, row_low = halves(fetched[pl.ds(owner_block * quarter, quarter)].reshape(quarter * cap, width))
        counted = slot_tally[owner_block]
        total = total + (dot(counted, row_high) + dot(counted, row_low))
    mean_high, mean_low = halves(total * scale)
    out_ref[...] = dot(mean_high, weight_high) + (dot(mean_high, weight_low) + dot(mean_low, weight_high))
    for group in range(4):
        for q in range(quarter):
            unless_own(peer_blocks[group], q, reply_copy(group, peer_blocks[group], q).wait_send)


def local(n, reps, features, seed_self, hub_ids, requests, counts, neighbors, weight, out_bias):
    rows, width = features.shape
    cap = requests.shape[1]
    hub_dev = hub_ids.shape[0]
    seeds = neighbors.shape[0]
    hbm = pl.BlockSpec(memory_space=pltpu.HBM)
    vmem = pl.BlockSpec(memory_space=pltpu.VMEM)
    dma = pltpu.SemaphoreType.DMA
    product = pl.pallas_call(
        functools.partial(kernel, n, reps),
        out_shape=jax.ShapeDtypeStruct((seeds, width), jnp.float32),
        in_specs=[hbm, hbm, vmem, vmem, vmem, vmem, hbm],
        out_specs=vmem,
        scratch_shapes=[
            pltpu.VMEM((rows, width), jnp.float32),
            pltpu.VMEM((seeds, width), jnp.float32),
            pltpu.VMEM(weight.shape, jnp.float32),
            pltpu.VMEM((4, n // 4, 1, LANES), jnp.int32),
            pltpu.VMEM((3, 4, n // 4, 1, LANES), jnp.int32),
            pltpu.VMEM((4, n // 4, 1, LANES), jnp.int32),
            pltpu.VMEM((4, n // 4, cap, width), jnp.float32),
            pltpu.VMEM((n, cap, width), jnp.float32),
            pltpu.VMEM((reps, hub_dev, width), jnp.float32),
            pltpu.VMEM((4, seeds, n // 4 * cap), jnp.bfloat16),
            dma((3,)),
            dma((6, n // 4)),
            dma((4, n // 4)),
            dma((2,)),
            dma((3,)),
            dma((4, n // 4)),
            dma((n,)),
            dma((reps,)),
            dma((reps,)),
        ],
        compiler_params=pltpu.CompilerParams(collective_id=0, has_side_effects=True),
    )(features, seed_self, hub_ids[None], requests, counts[None], neighbors.T, weight)
    return jnp.maximum(product + out_bias, 0.0)


def solution(mesh):
    return jax.shard_map(
        functools.partial(local, mesh.shape["shard"], mesh.shape["rep"]),
        mesh=mesh,
        in_specs=(
            P(("rep", "shard"), None),
            P(("rep", "shard"), None),
            P(("rep", "shard")),
            P(("rep", "shard"), None),
            P(("rep", "shard")),
            P(("rep", "shard"), None),
            P(),
            P(),
        ),
        out_specs=P(("rep", "shard"), None),
        check_vma=False,
    )
```

time: 26.6 us -> 26.1 us (0.981)
  the two profiles are of different devices: /device:TPU:9 before, /device:TPU:0 now
where the time goes in v3:
time: 26.1 us; the launch traced here: 25.9 us
  Pallas kernels  24.3 us (93%)
  other arithmetic  1.57 us (6%)
    pallas_call x1, Pallas kernels, local(): pl.pallas_call(functools.partial(kernel, n, reps), out_shape=jax.ShapeDty...  24.3 us
    max x1, other arithmetic, local(): return jnp.maximum(product + out_bias, 0.0)  1.57 us

profile of v3, /device:TPU:0, one launch (start us, length us, event | category | flops | bytes accessed | tf_op | source)
XLA Modules:
  0.0 25.9 jit_solution(9593564509565567492)
XLA Ops:
  0.0 0.0 copy-start
  0.0 24.3 %shard_map.82 = f32[128,256]{1,0:T(8,128)} custom-call(f32[512,256]{1,0:T(8,128)} %feat_hbm.1, f32[128,256]{1,0:T(8,128)} %self_hbm.1, s32[1,128]{1,0:T(1,128)} %bitcast.4, s32[16,32]{1,0:T(8,128)} %req_ref.1, s32[1,16]{1,0:T(1,128)} %bitcast.5, s32[15,128]{1,0:T(8,128)} %bitcast.3, f32[256,256]{1,0:T(8,128)} %weight_hbm.1), custom_call_target="tpu_custom_call" | custom-call | tf_op jit(solution)/shard_map/pallas_call | solution.py:266
  24.3 0.0 copy-done
  24.4 1.6 %add_maximum_fusion = f32[128,256]{1,0:T(8,128)} fusion(f32[128,256]{1,0:T(8,128)} %shard_map.82, f32[256]{0:T(256)S(1)} %copy-done), kind=kLoop, calls=%fused_computation | loop fusion | flops 65536 | bytes 263168 | tf_op jit(solution)/shard_map/max | solution.py:294
Async XLA Ops:
  0.0 24.3 %copy-start = (f32[256]{0:T(256)S(1)}, f32[256]{0:T(256)}, u32[]{:S(2)}) copy-start(f32[256]{0:T(256)} %param.15) | copy-start | bytes 3076

commit v4 on v3

--- a/solution.py
+++ b/solution.py
@@ -172,9 +172,10 @@
         for q in range(quarter):
             unless_own(peer_block, q, reply_copy(group, peer_block, q).start)
 
-    peer_blocks = (near, edge, 2 - lax.rem(block, 2), far)
-    own_group = 1 + inner
-    for group in range(3):
+    apart = 2 - lax.rem(block, 2)
+    peer_blocks = (near, inner * edge + (1 - inner) * apart, far, block)
+    own_group = 3
+    for group in range(2):
         answer(group, peer_blocks[group])
 
     @pl.when(is_inner)
@@ -182,7 +183,8 @@
         table_wait(2)
         start(passed[2])
 
-    answer(3, peer_blocks[3])
+    for group in range(2, 4):
+        answer(group, peer_blocks[group])
     fetched[me] = gathered[own_group, place]
 
     hub_columns = columns_of(jnp.broadcast_to(hub_ref[...], (8, hub_dev)))

time: 26.1 us -> 26.1 us (level)
  no operation moved by 1% of the time
where the time goes in v4:
time: 26.1 us; the launch traced here: 25.9 us
  Pallas kernels  24.3 us (93%)
  other arithmetic  1.57 us (6%)
    pallas_call x1, Pallas kernels, local(): pl.pallas_call(functools.partial(kernel, n, reps), out_shape=jax.ShapeDty...  24.3 us
    max x1, other arithmetic, local(): return jnp.maximum(product + out_bias, 0.0)  1.57 us

profile of v4, /device:TPU:0, one launch (start us, length us, event | category | flops | bytes accessed | tf_op | source)
XLA Modules:
  0.0 25.9 jit_solution(17004192991334163987)
XLA Ops:
  0.0 0.0 copy-start
  0.0 24.3 %shard_map.82 = f32[128,256]{1,0:T(8,128)} custom-call(f32[512,256]{1,0:T(8,128)} %feat_hbm.1, f32[128,256]{1,0:T(8,128)} %self_hbm.1, s32[1,128]{1,0:T(1,128)} %bitcast.4, s32[16,32]{1,0:T(8,128)} %req_ref.1, s32[1,16]{1,0:T(1,128)} %bitcast.5, s32[15,128]{1,0:T(8,128)} %bitcast.3, f32[256,256]{1,0:T(8,128)} %weight_hbm.1), custom_call_target="tpu_custom_call" | custom-call | tf_op jit(solution)/shard_map/pallas_call | solution.py:268
  24.3 0.0 copy-done
  24.4 1.6 %add_maximum_fusion = f32[128,256]{1,0:T(8,128)} fusion(f32[128,256]{1,0:T(8,128)} %shard_map.82, f32[256]{0:T(256)S(1)} %copy-done), kind=kLoop, calls=%fused_computation | loop fusion | flops 65536 | bytes 263168 | tf_op jit(solution)/shard_map/max | solution.py:296
Async XLA Ops:
  0.0 24.3 %copy-start = (f32[256]{0:T(256)S(1)}, f32[256]{0:T(256)}, u32[]{:S(2)}) copy-start(f32[256]{0:T(256)} %param.15) | copy-start | bytes 3076
